TPU v7x, 256 devices: a whole 4x4x8 slice. The times are simulated.
256 devices in a mesh: cell: 64 (over z, y, core), inst: 4 (over x).
Axes of the slice: x: 4, y: 4, z: 8, core: 2. Of those that a mesh axis runs over, the one named last changes fastest.
Arguments:
- fine_residual: float32 [8, 6, 524288], P('inst', None, 'cell'), may hold values from -6 to 6
- fine_map: int32 [524288], P('cell'), may hold values from 0 to 15
- routes: int32 [64, 64], P('cell'), may hold values from 0 to 63, as said below
- receive_lists: int32 [64, 192], P('cell'), may hold values from 0 to 1023
- neighbours: int32 [6, 65536], P(None, 'cell'), may hold values from 0 to 1215, as said below
- face_weights: float32 [6, 65536], P(None, 'cell'), may hold values from 0.3 to 3
- spectral_coef: float32 [65536], P('cell'), may hold values from 0.2 to 1
- diag_extra: float32 [6, 65536], P(None, 'cell'), may hold values from 0.5 to 2
Outputs:
- fine_correction: float32 [8, 6, 524288], P('inst', None, 'cell')
- coarse_correction: float32 [8, 6, 65536], P('inst', None, 'cell')
Inputs may be any that keep to these rules, and one draw needn't show every extreme that they name: `routes`: in row p, the value p appears 64 - 2 * 4 times, and (p - 1) mod 64 and (p + 1) mod 64 appear 4 times each. `receive_lists`: row o, entries t * 32 to t * 32 + 31, list cells that partition o receives as halo from partition (o + d) mod 64, with d = t - 3 for t < 3 and d = t - 2 otherwise. `neighbours`: A value below 1024 is a cell of the own partition; a value x of 1024 or more is halo slot x - 1024.
All inputs are finite; a program needn't handle non-finite values.
Results may differ from a plain program's by a relative error of at most 0.0001.
Values sent between devices are 32-bit elements; how exact they have to be, the bound alone decides.
A program may use at most 64 MiB of HBM per device.

v0:
```python
import functools
import math

import jax
import jax.numpy as jnp
from jax import lax
from jax.experimental import pallas as pl
from jax.experimental.pallas import tpu as pltpu
from jax.sharding import PartitionSpec as P

INST = 8
HB_INST = 7
VARS = 6
NB = 6
BLK = 128
CB = 16
RAD = 3
HS = 32
ITERS = 6
PEERS = 2 * RAD
OFFSETS = [t - RAD if t < RAD else t - RAD + 1 for t in range(PEERS)]
SWEEPERS = 3
ROWS = 16
SEND = 256
MESH = pl.DeviceIdType.MESH
F32 = jnp.float32
BF16 = jnp.bfloat16
T_Q, T_R, T_H, T_L = 0, 96, 192, 288
T_S, T_D, T_END = 384, 432, 480


def spectral_value(distance):
    if distance == 0:
        return 0.0
    sign = -1.0 if distance % 2 else 1.0
    return 0.5 * sign / math.sin(math.pi * distance / HB_INST)


def split2(x):
    hi = x.astype(BF16)
    return hi, (x - hi.astype(F32)).astype(BF16)


def split3(x):
    hi = x.astype(BF16)
    rest = x - hi.astype(F32)
    mid = rest.astype(BF16)
    return hi, mid, (rest - mid.astype(F32)).astype(BF16)


def dot(a, b):
    return lax.dot_general(a, b, (((1,), (0,)), ((), ())), preferred_element_type=F32)


def dot_t(a, b):
    return lax.dot_general(a, b, (((1,), (1,)), ((), ())), preferred_element_type=F32)


def kernel(
    n_cell,
    fr, fm, rt, rl, nb, fw, sc, de,
    coarse_o, blocks_o,
    fr_v, fm_v, rt_s, rl_v, nb_v, fw_v, sc_v, de_v,
    inv_v, pos_v, perm, perm_t, yu,
    ysend, rx, rx0, rx7, lsend, lrx,
    table, stable, sel, wh, wl, coef,
    r_v, sg_v, di_v, base_v, x_v, xh_v,
    xsend, halo, xf, gx, gx0, gx7,
    in_sem,
    l_ss, l_rs, r_ss, r_rs, h_ss, h_rs, f_ss, f_rs,
):
    cell = lax.axis_index("cell")
    inst = lax.axis_index("inst")
    blocks = fm_v.shape[0]
    handed = blocks // 16
    cc = blocks * CB
    n_inst = 4

    def at_cell(d):
        return lax.rem(cell + (d + n_cell), n_cell)

    def copy_in(i, src, dst):
        c = pltpu.make_async_copy(src, dst, in_sem.at[i])
        c.start()
        return c

    c_rt = copy_in(0, rt, rt_s)
    c_fr = copy_in(1, fr, fr_v)
    c_fm = copy_in(2, fm, fm_v)
    c_rl = copy_in(3, rl, rl_v)
    c_nb = copy_in(4, nb, nb_v)
    c_fw = copy_in(5, fw, fw_v)
    c_sc = copy_in(6, sc, sc_v)
    c_de = copy_in(7, de, de_v)

    barrier = pltpu.get_barrier_semaphore()
    partners = 0
    for d in OFFSETS:
        pl.semaphore_signal(barrier, inc=1, device_id={"cell": at_cell(d), "inst": inst}, device_id_type=MESH)
        partners += 1
    for d in (0, -1, 1):
        for j in range(1, n_inst):
            pl.semaphore_signal(
                barrier, inc=1,
                device_id={"cell": at_cell(d), "inst": lax.rem(inst + j, n_inst)},
                device_id_type=MESH,
            )
            partners += 1

    c_rt.wait()
    group = lax.broadcasted_iota(jnp.int32, (8, BLK), 0) * 8 + lax.broadcasted_iota(jnp.int32, (8, BLK), 1) // CB

    def find(step, carry):
        c0, c1, c2, inv, fwd = carry
        for u in range(8):
            b = step * 8 + u
            rel = lax.rem(rt_s[0, b] - cell + n_cell, n_cell)
            is0 = rel == 1
            is1 = rel == 0
            pos = jnp.where(is0, c0, jnp.where(is1, c1, c2))
            c0 = c0 + jnp.where(is0, 1, 0)
            c1 = c1 + jnp.where(is1, 1, 0)
            c2 = c2 + jnp.where(is0 | is1, 0, 1)
            inv = jnp.where(group == pos, b, inv)
            fwd = jnp.where(group == b, pos, fwd)
        return c0, c1, c2, inv, fwd

    zero8 = jnp.zeros((8, BLK), jnp.int32)
    init = (jnp.int32(0), jnp.int32(handed), jnp.int32(blocks - handed), zero8, zero8)
    found = lax.fori_loop(0, blocks // 8, find, init)
    within = lax.rem(lax.broadcasted_iota(jnp.int32, (8, BLK), 1), CB)
    inv_v[...] = found[3] * CB + within
    pos_v[...] = found[4] * CB + within

    c_nb.wait()
    c_fw.wait()
    c_sc.wait()
    c_de.wait()
    ids = [jnp.broadcast_to(nb_v[s : s + 1, :], (8, cc)) for s in range(NB)]
    face = [jnp.broadcast_to(fw_v[s : s + 1, :], (8, cc)) for s in range(NB)]
    total = face[0]
    for s in range(1, NB):
        total = total + face[s]
    for s in range(NB):
        for o in range(s + 1, NB):
            same = ids[s] == ids[o]
            face[s] = face[s] + jnp.where(same, face[o], 0.0)
            ids[o] = jnp.where(same, 2047, ids[o])

    def twice(x):
        return jnp.concatenate([x, x], axis=0)

    for s in range(NB):
        rows = pl.ds(16 * s, 16)
        table[pl.ds(T_Q + 16 * s, 16), :] = twice((ids[s] // 256).astype(F32)).astype(BF16)
        table[pl.ds(T_R + 16 * s, 16), :] = twice((ids[s] % 256).astype(F32)).astype(BF16)
        hi, lo = split2(twice(face[s]))
        table[pl.ds(T_H + 16 * s, 16), :] = hi
        table[pl.ds(T_L + 16 * s, 16), :] = lo
    sig = jnp.broadcast_to(sc_v[0:1, :], (8, cc))
    pair = [
        jnp.where(inst == 0, de_v[v : v + 1, :], jnp.where(inst == 1, de_v[2 + v : 3 + v, :], de_v[4 + v : 5 + v, :]))
        for v in range(2)
    ]
    odd = lax.rem(lax.broadcasted_iota(jnp.int32, (8, cc), 0), 4) >= 2
    diag = total + 3.0 * sig + jnp.where(odd, jnp.broadcast_to(pair[1], (8, cc)), jnp.broadcast_to(pair[0], (8, cc)))
    for k, part in enumerate(split3(twice(sig))):
        table[pl.ds(T_S + 16 * k, 16), :] = part
    for k, part in enumerate(split3(twice(diag))):
        table[pl.ds(T_D + 16 * k, 16), :] = part
    sg_v[:, SEND:] = twice(sig)
    di_v[:, SEND:] = twice(1.0 / diag)

    row = lax.broadcasted_iota(jnp.int32, (ROWS, BLK), 0)
    row_n = 2 * (row // 4) + row % 2
    row_v = (row % 4) // 2
    live = [p for p in range(ROWS) if 2 * (p // 4) + p % 2 < HB_INST]
    for slot, p in enumerate(live):
        n, v = 2 * (p // 4) + p % 2, (p % 4) // 2
        value = jnp.zeros((ROWS, BLK), F32)
        for m in range(HB_INST):
            value = jnp.where((row_n == m) & (row_v == v), spectral_value(m - n), value)
        coef[slot] = value

    row16 = lax.broadcasted_iota(jnp.int32, (16, BLK), 0).astype(F32).astype(BF16)

    def permutation(src, dst):
        def one(tile, _):
            line = jnp.broadcast_to(src[pl.ds(tile, 1), :], (16, BLK))
            lanes = pl.ds(pl.multiple_of(tile * BLK, BLK), BLK)
            high = (line // 256).astype(F32).astype(BF16)
            low = lax.rem(line, 256).astype(F32).astype(BF16)
            for kt in range(cc // 256):
                at = jnp.where(high == jnp.asarray(kt, BF16), low, jnp.full_like(low, -1.0))
                for j in range(16):
                    hit = at == row16 + jnp.asarray(16.0 * j, BF16)
                    dst[256 * kt + 16 * j : 256 * kt + 16 * j + 16, lanes] = jnp.where(
                        hit, jnp.ones((16, BLK), BF16), jnp.zeros((16, BLK), BF16)
                    )
            return 0

        lax.fori_loop(0, cc // BLK, one, 0)

    permutation(inv_v, perm)

    c_fr.wait()
    c_fm.wait()
    kept = 2 * inst + 1 < HB_INST
    rows_of = lax.rem(lax.broadcasted_iota(jnp.int32, (BLK, BLK), 0), CB)
    block_of = lax.broadcasted_iota(jnp.int32, (16, BLK), 0) // 2 == lax.broadcasted_iota(jnp.int32, (16, BLK), 1) // CB
    drop = (lax.rem(lax.broadcasted_iota(jnp.int32, (2, BLK), 0), 2) == 0) | kept

    def restrict(tile, _):
        maps = [jnp.broadcast_to(fm_v[pl.ds(tile * 8 + e, 1), :], (CB, BLK)) for e in range(8)]
        onehot = jnp.where(rows_of == jnp.concatenate(maps, axis=0), 1.0, 0.0).astype(BF16)
        rows = pl.ds(pl.multiple_of(tile * 16, 16), 16)
        lanes = pl.ds(pl.multiple_of(tile * BLK, BLK), BLK)
        his, los = [], []
        for v in range(VARS):
            hi, lo = split2(fr_v[v, rows, :])
            his.append(hi)
            los.append(lo)
        got = dot_t(jnp.concatenate(his + los, axis=0), onehot)
        for v in range(VARS):
            both = jnp.where(block_of, got[16 * v : 16 * v + 16] + got[96 + 16 * v : 112 + 16 * v], 0.0)
            half = both[0:8] + both[8:16]
            half = half[0:4] + half[4:8]
            yu[v // 2, 2 * (v % 2) : 2 * (v % 2) + 2, lanes] = jnp.where(drop, half[0:2] + half[2:4], 0.0)
        return 0

    lax.fori_loop(0, cc // BLK, restrict, 0)
    terms = split3(jnp.concatenate([yu[0], yu[1], yu[2], yu[2]], axis=0))
    terms = jnp.concatenate(terms, axis=0)
    for nt in (0, cc // 256 - 1, *range(1, cc // 256 - 1)):
        got = dot(terms, perm[:, 256 * nt : 256 * nt + 256])
        got = got[0:16] + got[16:32] + got[32:48]
        for g in range(SWEEPERS):
            ysend[g, :, 256 * nt : 256 * nt + 256] = got[4 * g : 4 * g + 4, :]

    c_rl.wait()
    lsend[...] = jnp.zeros_like(lsend)
    lsend[:, : PEERS * HS] = rl_v[...]

    pl.semaphore_wait(barrier, partners)

    def list_copy(t, target_cell):
        return pltpu.make_async_remote_copy(
            src_ref=lsend, dst_ref=lrx.at[t], send_sem=l_ss.at[t], recv_sem=l_rs.at[t],
            device_id={"cell": target_cell, "inst": inst}, device_id_type=MESH,
        )

    def rest_copy(g, kind, src):
        lanes = (pl.ds(0, cc), pl.ds(0, BLK), pl.ds(cc - BLK, BLK))[kind]
        dst = (rx, rx0, rx7)[kind]
        return pltpu.make_async_remote_copy(
            src_ref=ysend.at[g, :, lanes], dst_ref=dst.at[src], send_sem=r_ss.at[kind, g], recv_sem=r_rs.at[kind, src],
            device_id={"cell": at_cell((0, 1, -1)[kind]), "inst": g}, device_id_type=MESH,
        )

    def halo_copy(k, t):
        return pltpu.make_async_remote_copy(
            src_ref=xsend.at[k, t // 4], dst_ref=halo.at[k, t], send_sem=h_ss.at[k, t], recv_sem=h_rs.at[k, t],
            device_id={"cell": at_cell(-OFFSETS[t]), "inst": inst}, device_id_type=MESH,
        )

    def back_copy(g, kind, src):
        lanes = (pl.ds(0, cc), pl.ds(0, BLK), pl.ds(cc - BLK, BLK))[kind]
        dst = (gx, gx0, gx7)[kind]
        return pltpu.make_async_remote_copy(
            src_ref=xf.at[g, :, lanes], dst_ref=dst.at[src], send_sem=f_ss.at[kind, g], recv_sem=f_rs.at[kind, src],
            device_id={"cell": at_cell((0, -1, 1)[kind]), "inst": g}, device_id_type=MESH,
        )

    sweeping = inst < SWEEPERS

    @pl.when(sweeping)
    def _():
        for t in range(PEERS):
            list_copy(t, at_cell(OFFSETS[t])).start()

    for kind in (1, 2):
        for g in range(SWEEPERS):
            rest_copy(g, kind, inst).start()
    for g in range(SWEEPERS):
        @pl.when(inst != g)
        def _():
            rest_copy(g, 0, inst).start()

        @pl.when(inst == g)
        def _():
            rx[g] = ysend[g]

    quarter = lax.broadcasted_iota(jnp.int32, (ROWS, BLK), 1) // HS

    def build(src, lane_tiles, first_tile):
        def one(m, _):
            lt, kt = m // 5, lax.rem(m, 5)
            s_lanes = pl.ds(pl.multiple_of(lt * BLK, BLK), BLK)
            d_lanes = pl.ds(pl.multiple_of((lt + first_tile) * BLK, BLK), BLK)
            kf = kt.astype(F32).astype(BF16)
            at = []
            for s in range(NB):
                q = src[pl.ds(T_Q + 16 * s, 16), s_lanes]
                r = src[pl.ds(T_R + 16 * s, 16), s_lanes]
                at.append(jnp.where(q == kf, r, jnp.full_like(r, -1.0)))
            hs = [src[pl.ds(T_H + 16 * s, 16), s_lanes] for s in range(NB)]
            ls = [src[pl.ds(T_L + 16 * s, 16), s_lanes] for s in range(NB)]
            for j in range(16):
                here = row16 + jnp.asarray(16.0 * j, BF16)
                h = jnp.zeros((16, BLK), BF16)
                low = jnp.zeros((16, BLK), BF16)
                for s in range(NB):
                    hit = at[s] == here
                    h = jnp.where(hit, hs[s], h)
                    low = jnp.where(hit, ls[s], low)
                k_rows = pl.ds(pl.multiple_of(kt * 256 + 16 * j, 16), 16)
                wh[k_rows, d_lanes] = h
                wl[k_rows, d_lanes] = low
            return 0

        lax.fori_loop(0, lane_tiles * 5, one, 0)

    def local_part(x_all):
        own_hi, own_lo = split2(x_all[:, SEND:])
        xh_v[0:16, :] = own_hi
        xh_v[16:32, :] = own_lo
        x_v[...] = x_all
        for nt in range((SEND + cc) // 256):
            lanes = pl.ds(256 * nt, 256)
            a = dot(xh_v[...], wh[0:cc, lanes])
            b = dot(xh_v[0:16, :], wl[0:cc, lanes])
            halves = []
            for e in range(2):
                part = pl.ds(256 * nt + 128 * e, 128)
                acc = jnp.zeros((ROWS, BLK), F32)
                for slot, p in enumerate(live):
                    acc = acc + coef[slot] * jnp.broadcast_to(x_v[p : p + 1, part], (ROWS, BLK))
                halves.append(acc)
            sx = jnp.concatenate(halves, axis=1)
            base_v[:, lanes] = r_v[:, lanes] - sg_v[:, lanes] * sx + (a[0:16] + a[16:32] + b)

    def halo_rows(k):
        for t in range(PEERS):
            halo_copy(k, t).wait_recv()
        first = halo[k, 0]
        for t in range(1, 4):
            first = jnp.where(quarter == t, halo[k, t], first)
        second = jnp.where(quarter == 0, halo[k, 4], jnp.where(quarter == 1, halo[k, 5], 0.0))
        hi, lo = split2(jnp.concatenate([first, second], axis=1))
        return jnp.concatenate([hi, lo], axis=0)

    def with_halo(rows, lanes):
        a = dot(rows, wh[cc : cc + 256, lanes])
        b = dot(rows[0:16], wl[cc : cc + 256, lanes])
        return (base_v[:, lanes] + (a[0:16] + a[16:32] + b)) * di_v[:, lanes]

    def send_halo(k, x_send):
        xsend[k, 0] = x_send[:, 0:BLK]
        xsend[k, 1] = x_send[:, BLK:SEND]
        for t in range(PEERS):
            halo_copy(k, t).start()

    @pl.when(sweeping)
    def _():
        build(table, cc // BLK, SEND // BLK)
        permutation(pos_v, perm_t)
        for t in range(PEERS):
            list_copy(t, at_cell(OFFSETS[t])).wait_recv()
        lane_slot = lax.broadcasted_iota(jnp.int32, (1, SEND), 1) // HS
        wanted = jnp.full((1, SEND), 4096, jnp.int32)
        for t in range(PEERS):
            wanted = jnp.where(lane_slot == t, lrx[t], wanted)
        for kt in range(cc // 256):
            rows256 = lax.broadcasted_iota(jnp.int32, (256, SEND), 0) + 256 * kt
            sel[256 * kt : 256 * kt + 256, :] = jnp.where(rows256 == wanted, 1.0, 0.0).astype(BF16)
        taken = dot(table[...], sel[...])
        stable[...] = taken[0:T_S].astype(BF16)
        used = lane_slot < PEERS
        sg_v[:, 0:SEND] = taken[T_S : T_S + 16] + taken[T_S + 16 : T_S + 32] + taken[T_S + 32 : T_S + 48]
        d_send = taken[T_D : T_D + 16] + taken[T_D + 16 : T_D + 32] + taken[T_D + 32 : T_D + 48]
        di_v[:, 0:SEND] = 1.0 / jnp.where(used, d_send, 1.0)
        build(stable, SEND // BLK, 0)

        for src in range(n_inst):
            for kind in (1, 2):
                rest_copy(0, kind, src).wait_recv()

            @pl.when(inst != src)
            def _():
                rest_copy(0, 0, src).wait_recv()

        lane = lax.broadcasted_iota(jnp.int32, (ROWS, BLK), 1)
        mine = jnp.concatenate([rx[src] for src in range(n_inst)], axis=0)
        low = jnp.concatenate([rx0[src] for src in range(n_inst)], axis=0)
        high = jnp.concatenate([rx7[src] for src in range(n_inst)], axis=0)
        edge = handed * CB
        rest = jnp.concatenate(
            [
                jnp.where(lane < edge, low, mine[:, 0:BLK]),
                mine[:, BLK : cc - BLK],
                jnp.where(lane >= BLK - edge, high, mine[:, cc - BLK :]),
            ],
            axis=1,
        )
        parts = dot(jnp.concatenate(split3(rest), axis=0), sel[...])
        r_send = parts[0:16] + parts[16:32] + parts[32:48]
        x_send = r_send * di_v[:, 0:SEND]
        send_halo(0, x_send)
        r_v[:, 0:SEND] = r_send
        r_v[:, SEND:] = rest
        local_part(jnp.concatenate([x_send, rest * di_v[:, SEND:]], axis=1))

        def sweep(k, _):
            rows = halo_rows(k)
            x_send = with_halo(rows, pl.ds(0, SEND))
            send_halo(k + 1, x_send)
            parts = [x_send]
            for nt in range(cc // 256):
                parts.append(with_halo(rows, pl.ds(SEND + 256 * nt, 256)))
            local_part(jnp.concatenate(parts, axis=1))
            return 0

        lax.fori_loop(0, ITERS - 1, sweep, 0)
        rows = halo_rows(ITERS - 1)
        for nt in (0, cc // 256 - 1, *range(1, cc // 256 - 1)):
            out = with_halo(rows, pl.ds(SEND + 256 * nt, 256))
            for g in range(n_inst):
                xf[g, :, 256 * nt : 256 * nt + 256] = out[4 * g : 4 * g + 4, :]
            if nt == cc // 256 - 1:
                for kind in (1, 2):
                    for g in range(n_inst):
                        back_copy(g, kind, inst).start()
        for g in range(n_inst):
            @pl.when(inst != g)
            def _():
                back_copy(g, 0, inst).start()

            @pl.when(inst == g)
            def _():
                if g < SWEEPERS:
                    gx[g] = xf[g]

    @pl.when(jnp.logical_not(sweeping))
    def _():
        permutation(pos_v, perm_t)

    lane4 = lax.broadcasted_iota(jnp.int32, (4, BLK), 1)
    edge = handed * CB
    placed = []
    for src in range(SWEEPERS):
        for kind in (1, 2):
            back_copy(0, kind, src).wait_recv()

        @pl.when(inst != src)
        def _():
            back_copy(0, 0, src).wait_recv()

        own = gx[src]
        first = jnp.where(lane4 < edge, gx0[src], own[:, 0:BLK])
        last = jnp.where(lane4 >= BLK - edge, gx7[src], own[:, cc - BLK :])
        coarse_o[src] = own
        placed.append(jnp.concatenate([first, own[:, BLK : cc - BLK], last], axis=1))
    terms = jnp.concatenate(split3(jnp.concatenate(placed + placed[2:], axis=0)), axis=0)
    for nt in range(cc // 256):
        got = dot(terms, perm_t[:, 256 * nt : 256 * nt + 256])
        got = got[0:16] + got[16:32] + got[32:48]
        for g in range(SWEEPERS):
            blocks_o[g, :, 256 * nt : 256 * nt + 256] = got[4 * g : 4 * g + 4, :]

    for kind in (1, 2):
        for g in range(SWEEPERS):
            rest_copy(g, kind, inst).wait_send()
    for g in range(SWEEPERS):
        @pl.when(inst != g)
        def _():
            rest_copy(g, 0, inst).wait_send()

    @pl.when(sweeping)
    def _():
        for t in range(PEERS):
            list_copy(t, at_cell(OFFSETS[t])).wait_send()
            for k in range(ITERS):
                halo_copy(k, t).wait_send()
        for g in range(n_inst):
            for kind in (1, 2):
                back_copy(g, kind, inst).wait_send()

            @pl.when(inst != g)
            def _():
                back_copy(g, 0, inst).wait_send()


def prolong(fm, coarse, blocks_x, fine_o, coarse_o):
    for v in range(VARS):
        coarse_o[v] = coarse[v // 2, 2 * (v % 2) : 2 * (v % 2) + 2, :]
    for tile in range(blocks_x.shape[2] // BLK):
        lanes = pl.ds(tile * BLK, BLK)
        for half in range(2):
            maps = [
                jnp.broadcast_to(fm[tile * 8 + 4 * half + e : tile * 8 + 4 * half + e + 1, :], (2, BLK)) + (4 * half + e) * CB
                for e in range(4)
            ]
            index = jnp.concatenate(maps, axis=0)
            rows = pl.ds(16 * tile + 8 * half, 8)
            for v in range(VARS):
                x = blocks_x[v // 2, 2 * (v % 2) : 2 * (v % 2) + 2, lanes]
                x = jnp.concatenate([x, x, x, x], axis=0)
                fine_o[v, rows, :] = jnp.take_along_axis(x, index, axis=1, mode="promise_in_bounds")


def body(n_cell, fine_residual, fine_map, routes, receive_lists, neighbours, face_weights, spectral_coef, diag_extra):
    inst_dev, var_count, fine_dev = fine_residual.shape
    blocks = fine_dev // BLK
    cc = blocks * CB
    lanes = SEND + cc
    vmem = pltpu.VMEM
    dma = pltpu.SemaphoreType.DMA
    any_spec = pl.BlockSpec(memory_space=pl.ANY)
    out_spec = pl.BlockSpec(memory_space=pltpu.VMEM)
    fine_rows = fine_residual.reshape(inst_dev, var_count, blocks, BLK).transpose(1, 2, 0, 3)
    fine_rows = fine_rows.reshape(var_count, blocks * inst_dev, BLK)
    cells_map = fine_map.reshape(blocks, BLK)
    coarse, in_blocks = pl.pallas_call(
        functools.partial(kernel, n_cell),
        out_shape=(
            jax.ShapeDtypeStruct((SWEEPERS, 4, cc), F32),
            jax.ShapeDtypeStruct((SWEEPERS, 4, cc), F32),
        ),
        in_specs=[any_spec] * 8,
        out_specs=(out_spec, out_spec),
        scratch_shapes=[
            vmem(fine_rows.shape, F32),
            vmem((blocks, BLK), jnp.int32),
            pltpu.SMEM((1, blocks), jnp.int32),
            vmem((1, PEERS * HS), jnp.int32),
            vmem((NB, cc), jnp.int32),
            vmem((NB, cc), F32),
            vmem((1, cc), F32),
            vmem((VARS, cc), F32),
            vmem((8, BLK), jnp.int32),
            vmem((8, BLK), jnp.int32),
            vmem((cc, cc), BF16),
            vmem((cc, cc), BF16),
            vmem((SWEEPERS, 4, cc), F32),
            vmem((SWEEPERS, 4, cc), F32),
            vmem((4, 4, cc), F32),
            vmem((4, 4, BLK), F32),
            vmem((4, 4, BLK), F32),
            vmem((1, SEND), jnp.int32),
            vmem((PEERS, 1, SEND), jnp.int32),
            vmem((T_END, cc), BF16),
            vmem((T_S, SEND), BF16),
            vmem((cc, SEND), BF16),
            vmem((cc + 256, lanes), BF16),
            vmem((cc + 256, lanes), BF16),
            vmem((2 * HB_INST, ROWS, BLK), F32),
            vmem((ROWS, lanes), F32),
            vmem((ROWS, lanes), F32),
            vmem((ROWS, lanes), F32),
            vmem((ROWS, lanes), F32),
            vmem((ROWS, lanes), F32),
            vmem((2 * ROWS, cc), BF16),
            vmem((ITERS, 2, ROWS, BLK), F32),
            vmem((ITERS, PEERS, ROWS, BLK), F32),
            vmem((4, 4, cc), F32),
            vmem((SWEEPERS, 4, cc), F32),
            vmem((SWEEPERS, 4, BLK), F32),
            vmem((SWEEPERS, 4, BLK), F32),
            dma((8,)),
            dma((PEERS,)),
            dma((PEERS,)),
            dma((3, SWEEPERS)),
            dma((3, 4)),
            dma((ITERS, PEERS)),
            dma((ITERS, PEERS)),
            dma((3, 4)),
            dma((3, SWEEPERS)),
        ],
        compiler_params=pltpu.CompilerParams(collective_id=0, has_side_effects=True),
        name="multigrid",
    )(
        fine_rows,
        cells_map,
        routes,
        receive_lists,
        neighbours,
        face_weights,
        spectral_coef.reshape(1, cc),
        diag_extra,
    )
    fine, coarse = pl.pallas_call(
        prolong,
        out_shape=(
            jax.ShapeDtypeStruct(fine_rows.shape, F32),
            jax.ShapeDtypeStruct((var_count, inst_dev, cc), F32),
        ),
        in_specs=[out_spec] * 3,
        out_specs=(out_spec, out_spec),
        name="prolong",
    )(cells_map, coarse, in_blocks)
    fine = fine.reshape(var_count, blocks, inst_dev, BLK).transpose(2, 0, 1, 3).reshape(inst_dev, var_count, fine_dev)
    return fine, coarse.transpose(1, 0, 2)


def solution(mesh):
    in_specs = (
        P("inst", None, "cell"),
        P("cell"),
        P("cell", None),
        P("cell", None),
        P(None, "cell"),
        P(None, "cell"),
        P("cell"),
        P(None, "cell"),
    )
    out_specs = (P("inst", None, "cell"), P("inst", None, "cell"))
    return jax.shard_map(
        functools.partial(body, mesh.shape["cell"]), mesh=mesh, in_specs=in_specs, out_specs=out_specs, check_vma=False
    )
```

profile of v0, /device:TPU:1, one launch (start us, length us, event | category | flops | bytes accessed | tf_op | source)
XLA Modules:
  0.0 53.9 jit_solution(5761487250944748743)
XLA Ops:
  0.6 51.5 %multigrid.1 = (f32[3,4,1024]{2,1,0:T(4,128)}, f32[3,4,1024]{2,1,0:T(4,128)}) custom-call(f32[6,128,128]{2,1,0:T(8,128)} %bitcast.13, s32[64,128]{1,0:T(8,128)} %bitcast.14, s32[1,64]{1,0:T(1,128)} %rt.1, s32[1,192]{1,0:T(1,128)} %rl.1, s32[6,1024]{1,0:T(8,128)} %nb.1, f32[6,1024]{1,0:T(8,128)} %fw.1, f32[1,1024]{1,0:T(1,128)} %bitcast.16, f32[6,1024]{1,0:T(8,128)} %de.1), custom_call_target="tpu_custom_call" | custom-call | tf_op jit(solution)/shard_map/multigrid/pallas_call | solution.py:523
  52.1 1.8 %prolong.1 = (f32[6,128,128]{2,1,0:T(8,128)}, f32[6,2,1024]{2,1,0:T(2,128)}) custom-call(s32[64,128]{1,0:T(8,128)} %bitcast.15, f32[3,4,1024]{2,1,0:T(4,128)} %get-tuple-element.6.coarse, f32[3,4,1024]{2,1,0:T(4,128)} %get-tuple-element.7.blocks_x), custom_call_target="tpu_custom_call" | custom-call | tf_op jit(solution)/shard_map/prolong/pallas_call | solution.py:591
where the time goes:
time: 54.1 us; the launch traced here: 53.9 us
  Pallas kernels  53.3 us (99%)
  between operations  0.64 us (1%)
    pallas_call x1, Pallas kernels, body(): pl.pallas_call(functools.partial(kernel, n_cell), out_shape=(jax.ShapeDty...  51.5 us
    pallas_call x1, Pallas kernels, body(): pl.pallas_call(prolong, out_shape=(jax.ShapeDtypeStruct(fine_rows.shape,...  1.81 us

commit v1 on v0

--- a/solution.py
+++ b/solution.py
@@ -62,12 +62,11 @@
     coarse_o, blocks_o,
     fr_v, fm_v, rt_s, rl_v, nb_v, fw_v, sc_v, de_v,
     inv_v, pos_v, perm, perm_t, yu,
-    ysend, rx, rx0, rx7, lsend, lrx,
+    ysend, rx, rxe, lsend, lrx,
     table, stable, sel, wh, wl, coef,
     r_v, sg_v, di_v, base_v, x_v, xh_v,
-    xsend, halo, xf, gx, gx0, gx7,
-    in_sem,
-    l_ss, l_rs, r_ss, r_rs, h_ss, h_rs, f_ss, f_rs,
+    xsend, halo, xf, gx, gxe,
+    in_sem, out_sem, list_sem, rest_sem, halo_sem, back_sem,
 ):
     cell = lax.axis_index("cell")
     inst = lax.axis_index("inst")
@@ -110,27 +109,143 @@
     c_rt.wait()
     group = lax.broadcasted_iota(jnp.int32, (8, BLK), 0) * 8 + lax.broadcasted_iota(jnp.int32, (8, BLK), 1) // CB
 
+    above = at_cell(1)
+
     def find(step, carry):
-        c0, c1, c2, inv, fwd = carry
+        c0, c1, inv, fwd = carry
         for u in range(8):
             b = step * 8 + u
-            rel = lax.rem(rt_s[0, b] - cell + n_cell, n_cell)
-            is0 = rel == 1
-            is1 = rel == 0
-            pos = jnp.where(is0, c0, jnp.where(is1, c1, c2))
+            route = rt_s[0, b]
+            is0 = route == above
+            is1 = route == cell
+            pos = jnp.where(is1, c1, jnp.where(is0, c0, blocks + b - c0 - c1))
             c0 = c0 + jnp.where(is0, 1, 0)
             c1 = c1 + jnp.where(is1, 1, 0)
-            c2 = c2 + jnp.where(is0 | is1, 0, 1)
             inv = jnp.where(group == pos, b, inv)
             fwd = jnp.where(group == b, pos, fwd)
-        return c0, c1, c2, inv, fwd
+        return c0, c1, inv, fwd
 
     zero8 = jnp.zeros((8, BLK), jnp.int32)
-    init = (jnp.int32(0), jnp.int32(handed), jnp.int32(blocks - handed), zero8, zero8)
-    found = lax.fori_loop(0, blocks // 8, find, init)
+    found = lax.fori_loop(0, blocks // 8, find, (jnp.int32(0), jnp.int32(handed), zero8, zero8))
     within = lax.rem(lax.broadcasted_iota(jnp.int32, (8, BLK), 1), CB)
-    inv_v[...] = found[3] * CB + within
-    pos_v[...] = found[4] * CB + within
+    inv_v[...] = found[2] * CB + within
+    pos_v[...] = found[3] * CB + within
+
+    row16 = lax.broadcasted_iota(jnp.int32, (16, BLK), 0).astype(F32).astype(BF16)
+
+    def permutation_tile(src, dst, tile):
+        line = jnp.broadcast_to(src[pl.ds(tile, 1), :], (16, BLK))
+        lanes = pl.ds(pl.multiple_of(tile * BLK, BLK), BLK)
+        high = (line // 256).astype(F32).astype(BF16)
+        low = lax.rem(line, 256).astype(F32).astype(BF16)
+        for kt in range(cc // 256):
+            at = jnp.where(high == jnp.asarray(kt, BF16), low, jnp.full_like(low, -1.0))
+            for j in range(16):
+                hit = at == row16 + jnp.asarray(16.0 * j, BF16)
+                dst[256 * kt + 16 * j : 256 * kt + 16 * j + 16, lanes] = jnp.where(
+                    hit, jnp.ones((16, BLK), BF16), jnp.zeros((16, BLK), BF16)
+                )
+
+    c_fr.wait()
+    c_fm.wait()
+    kept = 2 * inst + 1 < HB_INST
+    rows_of = lax.rem(lax.broadcasted_iota(jnp.int32, (BLK, BLK), 0), CB)
+    block_of = lax.broadcasted_iota(jnp.int32, (16, BLK), 0) // 2 == lax.broadcasted_iota(jnp.int32, (16, BLK), 1) // CB
+    drop = (lax.rem(lax.broadcasted_iota(jnp.int32, (2, BLK), 0), 2) == 0) | kept
+
+    def restrict(tile):
+        maps = [jnp.broadcast_to(fm_v[pl.ds(tile * 8 + e, 1), :], (CB, BLK)) for e in range(8)]
+        onehot = jnp.where(rows_of == jnp.concatenate(maps, axis=0), 1.0, 0.0).astype(BF16)
+        rows = pl.ds(pl.multiple_of(tile * 16, 16), 16)
+        lanes = pl.ds(pl.multiple_of(tile * BLK, BLK), BLK)
+        his, los = [], []
+        for v in range(VARS):
+            hi, lo = split2(fr_v[v, rows, :])
+            his.append(hi)
+            los.append(lo)
+        got = dot_t(jnp.concatenate(his + los, axis=0), onehot)
+        for v in range(VARS):
+            both = jnp.where(block_of, got[16 * v : 16 * v + 16] + got[96 + 16 * v : 112 + 16 * v], 0.0)
+            half = both[0:8] + both[8:16]
+            half = half[0:4] + half[4:8]
+            yu[v // 2, 2 * (v % 2) : 2 * (v % 2) + 2, lanes] = jnp.where(drop, half[0:2] + half[2:4], 0.0)
+
+    def restrict_some(step, _):
+        for u in range(4):
+            restrict(step * 4 + u)
+            permutation_tile(inv_v, perm, step * 4 + u)
+        return 0
+
+    lax.fori_loop(0, cc // BLK // 4, restrict_some, 0)
+    terms = split3(jnp.concatenate([yu[0], yu[1], yu[2], yu[2]], axis=0))
+    terms = jnp.concatenate(terms, axis=0)
+    for nt in (0, cc // 256 - 1, *range(1, cc // 256 - 1)):
+        got = dot(terms, perm[:, 256 * nt : 256 * nt + 256])
+        got = got[0:16] + got[16:32] + got[32:48]
+        for g in range(SWEEPERS):
+            ysend[g, :, 256 * nt : 256 * nt + 256] = got[4 * g : 4 * g + 4, :]
+
+    c_rl.wait()
+    lsend[...] = jnp.zeros_like(lsend)
+    lsend[:, : PEERS * HS] = rl_v[...]
+
+    pl.semaphore_wait(barrier, partners)
+
+    def taken_all(ref, sem):
+        pltpu.make_async_copy(ref, ref, sem).wait()
+
+    def list_copy(t):
+        return pltpu.make_async_remote_copy(
+            src_ref=lsend, dst_ref=lrx.at[t], send_sem=out_sem.at[0], recv_sem=list_sem.at[0],
+            device_id={"cell": at_cell(OFFSETS[t]), "inst": inst}, device_id_type=MESH,
+        )
+
+    def rest_copy(g, kind):
+        if kind == 0:
+            src, dst = ysend.at[g], rx.at[inst]
+        else:
+            src = ysend.at[g, :, pl.ds((0, cc - BLK)[kind - 1], BLK)]
+            dst = rxe.at[kind - 1, inst]
+        return pltpu.make_async_remote_copy(
+            src_ref=src, dst_ref=dst, send_sem=out_sem.at[1 + min(kind, 1)], recv_sem=rest_sem.at[min(kind, 1)],
+            device_id={"cell": at_cell((0, 1, -1)[kind]), "inst": g}, device_id_type=MESH,
+        )
+
+    def halo_copy(k, t):
+        return pltpu.make_async_remote_copy(
+            src_ref=xsend.at[k, t // 4], dst_ref=halo.at[k, t], send_sem=out_sem.at[3], recv_sem=halo_sem.at[k],
+            device_id={"cell": at_cell(-OFFSETS[t]), "inst": inst}, device_id_type=MESH,
+        )
+
+    def back_copy(g, kind):
+        if kind == 0:
+            src, dst = xf.at[g], gx.at[inst]
+        else:
+            src = xf.at[g, :, pl.ds((0, cc - BLK)[kind - 1], BLK)]
+            dst = gxe.at[kind - 1, inst]
+        return pltpu.make_async_remote_copy(
+            src_ref=src, dst_ref=dst, send_sem=out_sem.at[4 + min(kind, 1)], recv_sem=back_sem.at[min(kind, 1)],
+            device_id={"cell": at_cell((0, -1, 1)[kind]), "inst": g}, device_id_type=MESH,
+        )
+
+    sweeping = inst < SWEEPERS
+
+    @pl.when(sweeping)
+    def _():
+        for t in range(PEERS):
+            list_copy(t).start()
+
+    for kind in (1, 2):
+        for g in range(SWEEPERS):
+            rest_copy(g, kind).start()
+    for g in range(SWEEPERS):
+        @pl.when(inst != g)
+        def _():
+            rest_copy(g, 0).start()
+
+        @pl.when(inst == g)
+        def _():
+            rx[g] = ysend[g]
 
     c_nb.wait()
     c_fw.wait()
@@ -181,114 +296,6 @@
         for m in range(HB_INST):
             value = jnp.where((row_n == m) & (row_v == v), spectral_value(m - n), value)
         coef[slot] = value
-
-    row16 = lax.broadcasted_iota(jnp.int32, (16, BLK), 0).astype(F32).astype(BF16)
-
-    def permutation(src, dst):
-        def one(tile, _):
-            line = jnp.broadcast_to(src[pl.ds(tile, 1), :], (16, BLK))
-            lanes = pl.ds(pl.multiple_of(tile * BLK, BLK), BLK)
-            high = (line // 256).astype(F32).astype(BF16)
-            low = lax.rem(line, 256).astype(F32).astype(BF16)
-            for kt in range(cc // 256):
-                at = jnp.where(high == jnp.asarray(kt, BF16), low, jnp.full_like(low, -1.0))
-                for j in range(16):
-                    hit = at == row16 + jnp.asarray(16.0 * j, BF16)
-                    dst[256 * kt + 16 * j : 256 * kt + 16 * j + 16, lanes] = jnp.where(
-                        hit, jnp.ones((16, BLK), BF16), jnp.zeros((16, BLK), BF16)
-                    )
-            return 0
-
-        lax.fori_loop(0, cc // BLK, one, 0)
-
-    permutation(inv_v, perm)
-
-    c_fr.wait()
-    c_fm.wait()
-    kept = 2 * inst + 1 < HB_INST
-    rows_of = lax.rem(lax.broadcasted_iota(jnp.int32, (BLK, BLK), 0), CB)
-    block_of = lax.broadcasted_iota(jnp.int32, (16, BLK), 0) // 2 == lax.broadcasted_iota(jnp.int32, (16, BLK), 1) // CB
-    drop = (lax.rem(lax.broadcasted_iota(jnp.int32, (2, BLK), 0), 2) == 0) | kept
-
-    def restrict(tile, _):
-        maps = [jnp.broadcast_to(fm_v[pl.ds(tile * 8 + e, 1), :], (CB, BLK)) for e in range(8)]
-        onehot = jnp.where(rows_of == jnp.concatenate(maps, axis=0), 1.0, 0.0).astype(BF16)
-        rows = pl.ds(pl.multiple_of(tile * 16, 16), 16)
-        lanes = pl.ds(pl.multiple_of(tile * BLK, BLK), BLK)
-        his, los = [], []
-        for v in range(VARS):
-            hi, lo = split2(fr_v[v, rows, :])
-            his.append(hi)
-            los.append(lo)
-        got = dot_t(jnp.concatenate(his + los, axis=0), onehot)
-        for v in range(VARS):
-            both = jnp.where(block_of, got[16 * v : 16 * v + 16] + got[96 + 16 * v : 112 + 16 * v], 0.0)
-            half = both[0:8] + both[8:16]
-            half = half[0:4] + half[4:8]
-            yu[v // 2, 2 * (v % 2) : 2 * (v % 2) + 2, lanes] = jnp.where(drop, half[0:2] + half[2:4], 0.0)
-        return 0
-
-    lax.fori_loop(0, cc // BLK, restrict, 0)
-    terms = split3(jnp.concatenate([yu[0], yu[1], yu[2], yu[2]], axis=0))
-    terms = jnp.concatenate(terms, axis=0)
-    for nt in (0, cc // 256 - 1, *range(1, cc // 256 - 1)):
-        got = dot(terms, perm[:, 256 * nt : 256 * nt + 256])
-        got = got[0:16] + got[16:32] + got[32:48]
-        for g in range(SWEEPERS):
-            ysend[g, :, 256 * nt : 256 * nt + 256] = got[4 * g : 4 * g + 4, :]
-
-    c_rl.wait()
-    lsend[...] = jnp.zeros_like(lsend)
-    lsend[:, : PEERS * HS] = rl_v[...]
-
-    pl.semaphore_wait(barrier, partners)
-
-    def list_copy(t, target_cell):
-        return pltpu.make_async_remote_copy(
-            src_ref=lsend, dst_ref=lrx.at[t], send_sem=l_ss.at[t], recv_sem=l_rs.at[t],
-            device_id={"cell": target_cell, "inst": inst}, device_id_type=MESH,
-        )
-
-    def rest_copy(g, kind, src):
-        lanes = (pl.ds(0, cc), pl.ds(0, BLK), pl.ds(cc - BLK, BLK))[kind]
-        dst = (rx, rx0, rx7)[kind]
-        return pltpu.make_async_remote_copy(
-            src_ref=ysend.at[g, :, lanes], dst_ref=dst.at[src], send_sem=r_ss.at[kind, g], recv_sem=r_rs.at[kind, src],
-            device_id={"cell": at_cell((0, 1, -1)[kind]), "inst": g}, device_id_type=MESH,
-        )
-
-    def halo_copy(k, t):
-        return pltpu.make_async_remote_copy(
-            src_ref=xsend.at[k, t // 4], dst_ref=halo.at[k, t], send_sem=h_ss.at[k, t], recv_sem=h_rs.at[k, t],
-            device_id={"cell": at_cell(-OFFSETS[t]), "inst": inst}, device_id_type=MESH,
-        )
-
-    def back_copy(g, kind, src):
-        lanes = (pl.ds(0, cc), pl.ds(0, BLK), pl.ds(cc - BLK, BLK))[kind]
-        dst = (gx, gx0, gx7)[kind]
-        return pltpu.make_async_remote_copy(
-            src_ref=xf.at[g, :, lanes], dst_ref=dst.at[src], send_sem=f_ss.at[kind, g], recv_sem=f_rs.at[kind, src],
-            device_id={"cell": at_cell((0, -1, 1)[kind]), "inst": g}, device_id_type=MESH,
-        )
-
-    sweeping = inst < SWEEPERS
-
-    @pl.when(sweeping)
-    def _():
-        for t in range(PEERS):
-            list_copy(t, at_cell(OFFSETS[t])).start()
-
-    for kind in (1, 2):
-        for g in range(SWEEPERS):
-            rest_copy(g, kind, inst).start()
-    for g in range(SWEEPERS):
-        @pl.when(inst != g)
-        def _():
-            rest_copy(g, 0, inst).start()
-
-        @pl.when(inst == g)
-        def _():
-            rx[g] = ysend[g]
 
     quarter = lax.broadcasted_iota(jnp.int32, (ROWS, BLK), 1) // HS
 
@@ -318,7 +325,7 @@
                 wl[k_rows, d_lanes] = low
             return 0
 
-        lax.fori_loop(0, lane_tiles * 5, one, 0)
+        lax.fori_loop(*(5 * tile for tile in lane_tiles), one, 0)
 
     def local_part(x_all):
         own_hi, own_lo = split2(x_all[:, SEND:])
@@ -340,8 +347,7 @@
             base_v[:, lanes] = r_v[:, lanes] - sg_v[:, lanes] * sx + (a[0:16] + a[16:32] + b)
 
     def halo_rows(k):
-        for t in range(PEERS):
-            halo_copy(k, t).wait_recv()
+        taken_all(halo.at[k], halo_sem.at[k])
         first = halo[k, 0]
         for t in range(1, 4):
             first = jnp.where(quarter == t, halo[k, t], first)
@@ -362,10 +368,9 @@
 
     @pl.when(sweeping)
     def _():
-        build(table, cc // BLK, SEND // BLK)
-        permutation(pos_v, perm_t)
-        for t in range(PEERS):
-            list_copy(t, at_cell(OFFSETS[t])).wait_recv()
+        early = cc // BLK * 5 // 8
+        build(table, (0, early), SEND // BLK)
+        taken_all(lrx, list_sem.at[0])
         lane_slot = lax.broadcasted_iota(jnp.int32, (1, SEND), 1) // HS
         wanted = jnp.full((1, SEND), 4096, jnp.int32)
         for t in range(PEERS):
@@ -379,20 +384,12 @@
         sg_v[:, 0:SEND] = taken[T_S : T_S + 16] + taken[T_S + 16 : T_S + 32] + taken[T_S + 32 : T_S + 48]
         d_send = taken[T_D : T_D + 16] + taken[T_D + 16 : T_D + 32] + taken[T_D + 32 : T_D + 48]
         di_v[:, 0:SEND] = 1.0 / jnp.where(used, d_send, 1.0)
-        build(stable, SEND // BLK, 0)
-
-        for src in range(n_inst):
-            for kind in (1, 2):
-                rest_copy(0, kind, src).wait_recv()
-
-            @pl.when(inst != src)
-            def _():
-                rest_copy(0, 0, src).wait_recv()
-
+        taken_all(rxe, rest_sem.at[1])
+        taken_all(rx.at[0 : n_inst - 1], rest_sem.at[0])
         lane = lax.broadcasted_iota(jnp.int32, (ROWS, BLK), 1)
         mine = jnp.concatenate([rx[src] for src in range(n_inst)], axis=0)
-        low = jnp.concatenate([rx0[src] for src in range(n_inst)], axis=0)
-        high = jnp.concatenate([rx7[src] for src in range(n_inst)], axis=0)
+        low = jnp.concatenate([rxe[0, src] for src in range(n_inst)], axis=0)
+        high = jnp.concatenate([rxe[1, src] for src in range(n_inst)], axis=0)
         edge = handed * CB
         rest = jnp.concatenate(
             [
@@ -406,6 +403,8 @@
         r_send = parts[0:16] + parts[16:32] + parts[32:48]
         x_send = r_send * di_v[:, 0:SEND]
         send_halo(0, x_send)
+        build(table, (early, cc // BLK), SEND // BLK)
+        build(stable, (0, SEND // BLK), 0)
         r_v[:, 0:SEND] = r_send
         r_v[:, SEND:] = rest
         local_part(jnp.concatenate([x_send, rest * di_v[:, SEND:]], axis=1))
@@ -429,35 +428,40 @@
             if nt == cc // 256 - 1:
                 for kind in (1, 2):
                     for g in range(n_inst):
-                        back_copy(g, kind, inst).start()
+                        back_copy(g, kind).start()
         for g in range(n_inst):
             @pl.when(inst != g)
             def _():
-                back_copy(g, 0, inst).start()
+                back_copy(g, 0).start()
 
             @pl.when(inst == g)
             def _():
                 if g < SWEEPERS:
                     gx[g] = xf[g]
 
+    def permute_back(step, _):
+        for u in range(2):
+            permutation_tile(pos_v, perm_t, step * 2 + u)
+        return 0
+
+    lax.fori_loop(0, cc // BLK // 2, permute_back, 0)
+    taken_all(gxe, back_sem.at[1])
+
+    @pl.when(sweeping)
+    def _():
+        taken_all(gx.at[0 : SWEEPERS - 1], back_sem.at[0])
+
     @pl.when(jnp.logical_not(sweeping))
     def _():
-        permutation(pos_v, perm_t)
+        taken_all(gx, back_sem.at[0])
 
     lane4 = lax.broadcasted_iota(jnp.int32, (4, BLK), 1)
     edge = handed * CB
     placed = []
     for src in range(SWEEPERS):
-        for kind in (1, 2):
-            back_copy(0, kind, src).wait_recv()
-
-        @pl.when(inst != src)
-        def _():
-            back_copy(0, 0, src).wait_recv()
-
         own = gx[src]
-        first = jnp.where(lane4 < edge, gx0[src], own[:, 0:BLK])
-        last = jnp.where(lane4 >= BLK - edge, gx7[src], own[:, cc - BLK :])
+        first = jnp.where(lane4 < edge, gxe[0, src], own[:, 0:BLK])
+        last = jnp.where(lane4 >= BLK - edge, gxe[1, src], own[:, cc - BLK :])
         coarse_o[src] = own
         placed.append(jnp.concatenate([first, own[:, BLK : cc - BLK], last], axis=1))
     terms = jnp.concatenate(split3(jnp.concatenate(placed + placed[2:], axis=0)), axis=0)
@@ -467,27 +471,19 @@
         for g in range(SWEEPERS):
             blocks_o[g, :, 256 * nt : 256 * nt + 256] = got[4 * g : 4 * g + 4, :]
 
-    for kind in (1, 2):
-        for g in range(SWEEPERS):
-            rest_copy(g, kind, inst).wait_send()
-    for g in range(SWEEPERS):
-        @pl.when(inst != g)
-        def _():
-            rest_copy(g, 0, inst).wait_send()
+    taken_all(ysend.at[:, :, 0:256], out_sem.at[2])
 
     @pl.when(sweeping)
     def _():
-        for t in range(PEERS):
-            list_copy(t, at_cell(OFFSETS[t])).wait_send()
-            for k in range(ITERS):
-                halo_copy(k, t).wait_send()
-        for g in range(n_inst):
-            for kind in (1, 2):
-                back_copy(g, kind, inst).wait_send()
-
-            @pl.when(inst != g)
-            def _():
-                back_copy(g, 0, inst).wait_send()
+        taken_all(ysend.at[0 : SWEEPERS - 1], out_sem.at[1])
+        taken_all(lrx, out_sem.at[0])
+        taken_all(halo, out_sem.at[3])
+        taken_all(xf.at[0 : n_inst - 1], out_sem.at[4])
+        taken_all(xf.at[:, :, 0:256], out_sem.at[5])
+
+    @pl.when(jnp.logical_not(sweeping))
+    def _():
+        taken_all(ysend, out_sem.at[1])
 
 
 def prolong(fm, coarse, blocks_x, fine_o, coarse_o):
@@ -544,8 +540,7 @@
             vmem((SWEEPERS, 4, cc), F32),
             vmem((SWEEPERS, 4, cc), F32),
             vmem((4, 4, cc), F32),
-            vmem((4, 4, BLK), F32),
-            vmem((4, 4, BLK), F32),
+            vmem((2, 4, 4, BLK), F32),
             vmem((1, SEND), jnp.int32),
             vmem((PEERS, 1, SEND), jnp.int32),
             vmem((T_END, cc), BF16),
@@ -564,17 +559,13 @@
             vmem((ITERS, PEERS, ROWS, BLK), F32),
             vmem((4, 4, cc), F32),
             vmem((SWEEPERS, 4, cc), F32),
-            vmem((SWEEPERS, 4, BLK), F32),
-            vmem((SWEEPERS, 4, BLK), F32),
+            vmem((2, SWEEPERS, 4, BLK), F32),
             dma((8,)),
-            dma((PEERS,)),
-            dma((PEERS,)),
-            dma((3, SWEEPERS)),
-            dma((3, 4)),
-            dma((ITERS, PEERS)),
-            dma((ITERS, PEERS)),
-            dma((3, 4)),
-            dma((3, SWEEPERS)),
+            dma((6,)),
+            dma((1,)),
+            dma((2,)),
+            dma((ITERS,)),
+            dma((2,)),
         ],
         compiler_params=pltpu.CompilerParams(collective_id=0, has_side_effects=True),
         name="multigrid",

time: 54.1 us -> 50.6 us (0.935)
  Pallas kernels: 53.3 us -> 49.8 us
    pallas_call x1, Pallas kernels: 51.5 us -> 48 us  [body(): pl.pallas_call(functools.partial(kernel, n_cell), out_shape=(jax.ShapeDty...]
where the time goes in v1:
time: 50.6 us; the launch traced here: 50.5 us
  Pallas kernels  49.8 us (98%)
  between operations  0.64 us (1%)
    pallas_call x1, Pallas kernels, body(): pl.pallas_call(functools.partial(kernel, n_cell), out_shape=(jax.ShapeDty...  48 us
    pallas_call x1, Pallas kernels, body(): pl.pallas_call(prolong, out_shape=(jax.ShapeDtypeStruct(fine_rows.shape,...  1.81 us

profile of v1, /device:TPU:1, one launch (start us, length us, event | category | flops | bytes accessed | tf_op | source)
XLA Modules:
  0.0 50.5 jit_solution(14614808780848245387)
XLA Ops:
  0.6 48.0 %multigrid.1 = (f32[3,4,1024]{2,1,0:T(4,128)}, f32[3,4,1024]{2,1,0:T(4,128)}) custom-call(f32[6,128,128]{2,1,0:T(8,128)} %bitcast.13, s32[64,128]{1,0:T(8,128)} %bitcast.14, s32[1,64]{1,0:T(1,128)} %rt.1, s32[1,192]{1,0:T(1,128)} %rl.1, s32[6,1024]{1,0:T(8,128)} %nb.1, f32[6,1024]{1,0:T(8,128)} %fw.1, f32[1,1024]{1,0:T(1,128)} %bitcast.16, f32[6,1024]{1,0:T(8,128)} %de.1), custom_call_target="tpu_custom_call" | custom-call | tf_op jit(solution)/shard_map/multigrid/pallas_call | solution.py:519
  48.7 1.8 %prolong.1 = (f32[6,128,128]{2,1,0:T(8,128)}, f32[6,2,1024]{2,1,0:T(2,128)}) custom-call(s32[64,128]{1,0:T(8,128)} %bitcast.15, f32[3,4,1024]{2,1,0:T(4,128)} %get-tuple-element.6.coarse, f32[3,4,1024]{2,1,0:T(4,128)} %get-tuple-element.7.blocks_x), custom_call_target="tpu_custom_call" | custom-call | tf_op jit(solution)/shard_map/prolong/pallas_call | solution.py:582

commit v2 on v1

--- a/solution.py
+++ b/solution.py
@@ -25,8 +25,8 @@
 MESH = pl.DeviceIdType.MESH
 F32 = jnp.float32
 BF16 = jnp.bfloat16
-T_Q, T_R, T_H, T_L = 0, 96, 192, 288
-T_S, T_D, T_END = 384, 432, 480
+T_Q, T_R, T_H, T_L, T_END = 0, 6, 12, 18, 24
+PLANE, CORES = 8, 2
 
 
 def spectral_value(distance):
@@ -62,11 +62,11 @@
     coarse_o, blocks_o,
     fr_v, fm_v, rt_s, rl_v, nb_v, fw_v, sc_v, de_v,
     inv_v, pos_v, perm, perm_t, yu,
-    ysend, rx, rxe, lsend, lrx,
+    ysend, rx, rxe, lsend, lrx, dsend, drx, nb_r, fw_r,
     table, stable, sel, wh, wl, coef,
     r_v, sg_v, di_v, base_v, x_v, xh_v,
     xsend, halo, xf, gx, gxe,
-    in_sem, out_sem, list_sem, rest_sem, halo_sem, back_sem,
+    in_sem, out_sem, list_sem, move_sem, rest_sem, halo_sem, back_sem,
 ):
     cell = lax.axis_index("cell")
     inst = lax.axis_index("inst")
@@ -75,8 +75,16 @@
     cc = blocks * CB
     n_inst = 4
 
-    def at_cell(d):
-        return lax.rem(cell + (d + n_cell), n_cell)
+    def wrap(c):
+        return lax.rem(c + n_cell, n_cell)
+
+    def mirror(c):
+        z, place = lax.div(c, PLANE), lax.rem(c, PLANE)
+        core = lax.rem(place, CORES)
+        return jnp.where(lax.rem(z, 2) == 1, z * PLANE + (PLANE - CORES) - (place - core) + core, c)
+
+    me = mirror(cell)
+    swapped = me != cell
 
     def copy_in(i, src, dst):
         c = pltpu.make_async_copy(src, dst, in_sem.at[i])
@@ -93,23 +101,42 @@
     c_de = copy_in(7, de, de_v)
 
     barrier = pltpu.get_barrier_semaphore()
-    partners = 0
+
+    def greet(c, i):
+        pl.semaphore_signal(barrier, inc=1, device_id={"cell": c, "inst": i}, device_id_type=MESH)
+
+    def others(c):
+        for j in range(n_inst):
+            greet(c, lax.rem(inst + j, n_inst))
+
+    partners = jnp.int32(3)
+    for j in range(1, n_inst):
+        greet(me, lax.rem(inst + j, n_inst))
+
+    @pl.when(swapped)
+    def _():
+        greet(me, inst)
+
+    partners = partners + jnp.where(swapped, 1, 0)
+    for d in (-1, 1):
+        others(mirror(wrap(cell + d)))
+        others(wrap(me + d))
+        partners = partners + 2 * n_inst
+    for d in (-3, -2, 2, 3):
+        for target in (mirror(wrap(cell + d)), wrap(me - d)):
+            @pl.when(target != cell)
+            def _():
+                greet(target, inst)
+
+            partners = partners + jnp.where(target != cell, 1, 0)
     for d in OFFSETS:
-        pl.semaphore_signal(barrier, inc=1, device_id={"cell": at_cell(d), "inst": inst}, device_id_type=MESH)
-        partners += 1
-    for d in (0, -1, 1):
-        for j in range(1, n_inst):
-            pl.semaphore_signal(
-                barrier, inc=1,
-                device_id={"cell": at_cell(d), "inst": lax.rem(inst + j, n_inst)},
-                device_id_type=MESH,
-            )
-            partners += 1
+        greet(mirror(wrap(me + d)), inst)
+        partners = partners + 1
 
     c_rt.wait()
     group = lax.broadcasted_iota(jnp.int32, (8, BLK), 0) * 8 + lax.broadcasted_iota(jnp.int32, (8, BLK), 1) // CB
 
-    above = at_cell(1)
+    above = wrap(cell + 1)
 
     def find(step, carry):
         c0, c1, inv, fwd = carry
@@ -189,6 +216,22 @@
     lsend[...] = jnp.zeros_like(lsend)
     lsend[:, : PEERS * HS] = rl_v[...]
 
+    c_nb.wait()
+    c_fw.wait()
+    c_sc.wait()
+    c_de.wait()
+    total = fw_v[0:1, :]
+    for s in range(1, NB):
+        total = total + fw_v[s : s + 1, :]
+    total = total + 3.0 * sc_v[...]
+    for v in range(2):
+        extra = jnp.where(
+            inst == 0, de_v[v : v + 1, :], jnp.where(inst == 1, de_v[2 + v : 3 + v, :], de_v[4 + v : 5 + v, :])
+        )
+        dsend[v : v + 1, :] = total + extra
+    dsend[2:3, :] = sc_v[...]
+    dsend[3:4, :] = sc_v[...]
+
     pl.semaphore_wait(barrier, partners)
 
     def taken_all(ref, sem):
@@ -197,8 +240,25 @@
     def list_copy(t):
         return pltpu.make_async_remote_copy(
             src_ref=lsend, dst_ref=lrx.at[t], send_sem=out_sem.at[0], recv_sem=list_sem.at[0],
-            device_id={"cell": at_cell(OFFSETS[t]), "inst": inst}, device_id_type=MESH,
+            device_id={"cell": mirror(wrap(cell + OFFSETS[t])), "inst": inst}, device_id_type=MESH,
         )
+
+    moves = ((dsend, drx), (nb_v, nb_r), (fw_v, fw_r))
+
+    def move_copy(m):
+        return pltpu.make_async_remote_copy(
+            src_ref=moves[m][0], dst_ref=moves[m][1], send_sem=out_sem.at[6 + m], recv_sem=move_sem.at[m],
+            device_id={"cell": me, "inst": inst}, device_id_type=MESH,
+        )
+
+    def move(m):
+        @pl.when(swapped)
+        def _():
+            move_copy(m).start()
+
+        @pl.when(jnp.logical_not(swapped))
+        def _():
+            pltpu.make_async_copy(*moves[m], move_sem.at[m]).start()
 
     def rest_copy(g, kind):
         if kind == 0:
@@ -208,13 +268,13 @@
             dst = rxe.at[kind - 1, inst]
         return pltpu.make_async_remote_copy(
             src_ref=src, dst_ref=dst, send_sem=out_sem.at[1 + min(kind, 1)], recv_sem=rest_sem.at[min(kind, 1)],
-            device_id={"cell": at_cell((0, 1, -1)[kind]), "inst": g}, device_id_type=MESH,
+            device_id={"cell": mirror(wrap(cell + (0, 1, -1)[kind])), "inst": g}, device_id_type=MESH,
         )
 
     def halo_copy(k, t):
         return pltpu.make_async_remote_copy(
             src_ref=xsend.at[k, t // 4], dst_ref=halo.at[k, t], send_sem=out_sem.at[3], recv_sem=halo_sem.at[k],
-            device_id={"cell": at_cell(-OFFSETS[t]), "inst": inst}, device_id_type=MESH,
+            device_id={"cell": mirror(wrap(me - OFFSETS[t])), "inst": inst}, device_id_type=MESH,
         )
 
     def back_copy(g, kind):
@@ -225,7 +285,7 @@
             dst = gxe.at[kind - 1, inst]
         return pltpu.make_async_remote_copy(
             src_ref=src, dst_ref=dst, send_sem=out_sem.at[4 + min(kind, 1)], recv_sem=back_sem.at[min(kind, 1)],
-            device_id={"cell": at_cell((0, -1, 1)[kind]), "inst": g}, device_id_type=MESH,
+            device_id={"cell": wrap(me + (0, -1, 1)[kind]), "inst": g}, device_id_type=MESH,
         )
 
     sweeping = inst < SWEEPERS
@@ -233,58 +293,42 @@
     @pl.when(sweeping)
     def _():
         for t in range(PEERS):
-            list_copy(t).start()
+            if abs(OFFSETS[t]) == 2:
+                here = mirror(wrap(cell + OFFSETS[t])) == cell
+
+                @pl.when(here)
+                def _():
+                    pltpu.make_async_copy(lsend, lrx.at[t], list_sem.at[0]).start()
+
+                @pl.when(jnp.logical_not(here))
+                def _():
+                    list_copy(t).start()
+            else:
+                list_copy(t).start()
 
     for kind in (1, 2):
         for g in range(SWEEPERS):
             rest_copy(g, kind).start()
+
+    @pl.when(sweeping)
+    def _():
+        move(0)
+
     for g in range(SWEEPERS):
-        @pl.when(inst != g)
+        local = (inst == g) & jnp.logical_not(swapped)
+
+        @pl.when(jnp.logical_not(local))
         def _():
             rest_copy(g, 0).start()
 
-        @pl.when(inst == g)
+        @pl.when(local)
         def _():
-            rx[g] = ysend[g]
-
-    c_nb.wait()
-    c_fw.wait()
-    c_sc.wait()
-    c_de.wait()
-    ids = [jnp.broadcast_to(nb_v[s : s + 1, :], (8, cc)) for s in range(NB)]
-    face = [jnp.broadcast_to(fw_v[s : s + 1, :], (8, cc)) for s in range(NB)]
-    total = face[0]
-    for s in range(1, NB):
-        total = total + face[s]
-    for s in range(NB):
-        for o in range(s + 1, NB):
-            same = ids[s] == ids[o]
-            face[s] = face[s] + jnp.where(same, face[o], 0.0)
-            ids[o] = jnp.where(same, 2047, ids[o])
-
-    def twice(x):
-        return jnp.concatenate([x, x], axis=0)
-
-    for s in range(NB):
-        rows = pl.ds(16 * s, 16)
-        table[pl.ds(T_Q + 16 * s, 16), :] = twice((ids[s] // 256).astype(F32)).astype(BF16)
-        table[pl.ds(T_R + 16 * s, 16), :] = twice((ids[s] % 256).astype(F32)).astype(BF16)
-        hi, lo = split2(twice(face[s]))
-        table[pl.ds(T_H + 16 * s, 16), :] = hi
-        table[pl.ds(T_L + 16 * s, 16), :] = lo
-    sig = jnp.broadcast_to(sc_v[0:1, :], (8, cc))
-    pair = [
-        jnp.where(inst == 0, de_v[v : v + 1, :], jnp.where(inst == 1, de_v[2 + v : 3 + v, :], de_v[4 + v : 5 + v, :]))
-        for v in range(2)
-    ]
-    odd = lax.rem(lax.broadcasted_iota(jnp.int32, (8, cc), 0), 4) >= 2
-    diag = total + 3.0 * sig + jnp.where(odd, jnp.broadcast_to(pair[1], (8, cc)), jnp.broadcast_to(pair[0], (8, cc)))
-    for k, part in enumerate(split3(twice(sig))):
-        table[pl.ds(T_S + 16 * k, 16), :] = part
-    for k, part in enumerate(split3(twice(diag))):
-        table[pl.ds(T_D + 16 * k, 16), :] = part
-    sg_v[:, SEND:] = twice(sig)
-    di_v[:, SEND:] = twice(1.0 / diag)
+            pltpu.make_async_copy(ysend.at[g], rx.at[g], rest_sem.at[0]).start()
+
+    @pl.when(sweeping)
+    def _():
+        move(1)
+        move(2)
 
     row = lax.broadcasted_iota(jnp.int32, (ROWS, BLK), 0)
     row_n = 2 * (row // 4) + row % 2
@@ -306,12 +350,14 @@
             d_lanes = pl.ds(pl.multiple_of((lt + first_tile) * BLK, BLK), BLK)
             kf = kt.astype(F32).astype(BF16)
             at = []
+            def line(i):
+                return jnp.broadcast_to(src[i : i + 1, s_lanes], (16, BLK)).astype(BF16)
+
             for s in range(NB):
-                q = src[pl.ds(T_Q + 16 * s, 16), s_lanes]
-                r = src[pl.ds(T_R + 16 * s, 16), s_lanes]
-                at.append(jnp.where(q == kf, r, jnp.full_like(r, -1.0)))
-            hs = [src[pl.ds(T_H + 16 * s, 16), s_lanes] for s in range(NB)]
-            ls = [src[pl.ds(T_L + 16 * s, 16), s_lanes] for s in range(NB)]
+                r = line(T_R + s)
+                at.append(jnp.where(line(T_Q + s) == kf, r, jnp.full_like(r, -1.0)))
+            hs = [line(T_H + s) for s in range(NB)]
+            ls = [line(T_L + s) for s in range(NB)]
             for j in range(16):
                 here = row16 + jnp.asarray(16.0 * j, BF16)
                 h = jnp.zeros((16, BLK), BF16)
@@ -368,8 +414,28 @@
 
     @pl.when(sweeping)
     def _():
-        early = cc // BLK * 5 // 8
-        build(table, (0, early), SEND // BLK)
+        def own_matrix():
+            taken_all(nb_r, move_sem.at[1])
+            taken_all(fw_r, move_sem.at[2])
+            ids = [jnp.broadcast_to(nb_r[s : s + 1, :], (8, cc)) for s in range(NB)]
+            face = [jnp.broadcast_to(fw_r[s : s + 1, :], (8, cc)) for s in range(NB)]
+            for s in range(NB):
+                for o in range(s + 1, NB):
+                    same = ids[s] == ids[o]
+                    face[s] = face[s] + jnp.where(same, face[o], 0.0)
+                    ids[o] = jnp.where(same, 2047, ids[o])
+            for s in range(NB):
+                table[T_Q + s : T_Q + s + 1, :] = lax.shift_right_logical(ids[s], 8).astype(F32)[0:1]
+                table[T_R + s : T_R + s + 1, :] = (ids[s] & 255).astype(F32)[0:1]
+                hi = face[s].astype(BF16).astype(F32)
+                table[T_H + s : T_H + s + 1, :] = hi[0:1]
+                table[T_L + s : T_L + s + 1, :] = (face[s] - hi).astype(BF16).astype(F32)[0:1]
+            build(table, (0, cc // BLK), SEND // BLK)
+
+        @pl.when(jnp.logical_not(swapped))
+        def _():
+            own_matrix()
+
         taken_all(lrx, list_sem.at[0])
         lane_slot = lax.broadcasted_iota(jnp.int32, (1, SEND), 1) // HS
         wanted = jnp.full((1, SEND), 4096, jnp.int32)
@@ -378,14 +444,21 @@
         for kt in range(cc // 256):
             rows256 = lax.broadcasted_iota(jnp.int32, (256, SEND), 0) + 256 * kt
             sel[256 * kt : 256 * kt + 256, :] = jnp.where(rows256 == wanted, 1.0, 0.0).astype(BF16)
-        taken = dot(table[...], sel[...])
-        stable[...] = taken[0:T_S].astype(BF16)
+        taken_all(drx, move_sem.at[0])
+        late = dot(jnp.concatenate(split3(jnp.concatenate([drx[...], drx[...]], axis=0)), axis=0), sel[...])
+        late = late[0:8] + late[8:16] + late[16:24]
+
+        def by_variable(x, width):
+            second = lax.rem(lax.broadcasted_iota(jnp.int32, (ROWS, width), 0), 4) >= 2
+            return jnp.where(second, jnp.broadcast_to(x[1:2], (ROWS, width)), jnp.broadcast_to(x[0:1], (ROWS, width)))
+
         used = lane_slot < PEERS
-        sg_v[:, 0:SEND] = taken[T_S : T_S + 16] + taken[T_S + 16 : T_S + 32] + taken[T_S + 32 : T_S + 48]
-        d_send = taken[T_D : T_D + 16] + taken[T_D + 16 : T_D + 32] + taken[T_D + 32 : T_D + 48]
-        di_v[:, 0:SEND] = 1.0 / jnp.where(used, d_send, 1.0)
+        sg_v[:, 0:SEND] = jnp.broadcast_to(late[2:3], (ROWS, SEND))
+        di_v[:, 0:SEND] = 1.0 / jnp.where(used, by_variable(late, SEND), 1.0)
+        sg_v[:, SEND:] = jnp.broadcast_to(drx[2:3, :], (ROWS, cc))
+        di_v[:, SEND:] = 1.0 / by_variable(drx[...], cc)
         taken_all(rxe, rest_sem.at[1])
-        taken_all(rx.at[0 : n_inst - 1], rest_sem.at[0])
+        taken_all(rx, rest_sem.at[0])
         lane = lax.broadcasted_iota(jnp.int32, (ROWS, BLK), 1)
         mine = jnp.concatenate([rx[src] for src in range(n_inst)], axis=0)
         low = jnp.concatenate([rxe[0, src] for src in range(n_inst)], axis=0)
@@ -403,7 +476,12 @@
         r_send = parts[0:16] + parts[16:32] + parts[32:48]
         x_send = r_send * di_v[:, 0:SEND]
         send_halo(0, x_send)
-        build(table, (early, cc // BLK), SEND // BLK)
+
+        @pl.when(swapped)
+        def _():
+            own_matrix()
+
+        stable[...] = dot(table[...].astype(BF16), sel[...])
         build(stable, (0, SEND // BLK), 0)
         r_v[:, 0:SEND] = r_send
         r_v[:, SEND:] = rest
@@ -430,14 +508,16 @@
                     for g in range(n_inst):
                         back_copy(g, kind).start()
         for g in range(n_inst):
-            @pl.when(inst != g)
+            local = (inst == g) & jnp.logical_not(swapped)
+
+            @pl.when(jnp.logical_not(local))
             def _():
                 back_copy(g, 0).start()
 
-            @pl.when(inst == g)
-            def _():
-                if g < SWEEPERS:
-                    gx[g] = xf[g]
+            if g < SWEEPERS:
+                @pl.when(local)
+                def _():
+                    pltpu.make_async_copy(xf.at[g], gx.at[g], back_sem.at[0]).start()
 
     def permute_back(step, _):
         for u in range(2):
@@ -446,15 +526,7 @@
 
     lax.fori_loop(0, cc // BLK // 2, permute_back, 0)
     taken_all(gxe, back_sem.at[1])
-
-    @pl.when(sweeping)
-    def _():
-        taken_all(gx.at[0 : SWEEPERS - 1], back_sem.at[0])
-
-    @pl.when(jnp.logical_not(sweeping))
-    def _():
-        taken_all(gx, back_sem.at[0])
-
+    taken_all(gx, back_sem.at[0])
     lane4 = lax.broadcasted_iota(jnp.int32, (4, BLK), 1)
     edge = handed * CB
     placed = []
@@ -473,17 +545,35 @@
 
     taken_all(ysend.at[:, :, 0:256], out_sem.at[2])
 
+    @pl.when(sweeping & jnp.logical_not(swapped))
+    def _():
+        taken_all(ysend.at[0 : SWEEPERS - 1], out_sem.at[1])
+        taken_all(xf.at[0 : n_inst - 1], out_sem.at[4])
+
+    @pl.when(jnp.logical_not(sweeping) | swapped)
+    def _():
+        taken_all(ysend, out_sem.at[1])
+
+    @pl.when(sweeping & swapped)
+    def _():
+        taken_all(xf, out_sem.at[4])
+        for m in range(3):
+            taken_all(moves[m][1], out_sem.at[6 + m])
+
     @pl.when(sweeping)
     def _():
-        taken_all(ysend.at[0 : SWEEPERS - 1], out_sem.at[1])
-        taken_all(lrx, out_sem.at[0])
+        at_home = (mirror(wrap(cell + 2)) == cell) | (mirror(wrap(cell - 2)) == cell)
+
+        @pl.when(at_home)
+        def _():
+            taken_all(lrx.at[0 : PEERS - 1], out_sem.at[0])
+
+        @pl.when(jnp.logical_not(at_home))
+        def _():
+            taken_all(lrx, out_sem.at[0])
+
         taken_all(halo, out_sem.at[3])
-        taken_all(xf.at[0 : n_inst - 1], out_sem.at[4])
         taken_all(xf.at[:, :, 0:256], out_sem.at[5])
-
-    @pl.when(jnp.logical_not(sweeping))
-    def _():
-        taken_all(ysend, out_sem.at[1])
 
 
 def prolong(fm, coarse, blocks_x, fine_o, coarse_o):
@@ -543,8 +633,12 @@
             vmem((2, 4, 4, BLK), F32),
             vmem((1, SEND), jnp.int32),
             vmem((PEERS, 1, SEND), jnp.int32),
-            vmem((T_END, cc), BF16),
-            vmem((T_S, SEND), BF16),
+            vmem((4, cc), F32),
+            vmem((4, cc), F32),
+            vmem((NB, cc), jnp.int32),
+            vmem((NB, cc), F32),
+            vmem((T_END, cc), F32),
+            vmem((T_END, SEND), F32),
             vmem((cc, SEND), BF16),
             vmem((cc + 256, lanes), BF16),
             vmem((cc + 256, lanes), BF16),
@@ -561,8 +655,9 @@
             vmem((SWEEPERS, 4, cc), F32),
             vmem((2, SWEEPERS, 4, BLK), F32),
             dma((8,)),
-            dma((6,)),
+            dma((9,)),
             dma((1,)),
+            dma((3,)),
             dma((2,)),
             dma((ITERS,)),
             dma((2,)),

time: 50.6 us -> 46.5 us (0.919)
  Pallas kernels: 49.8 us -> 45.7 us
    pallas_call x1, Pallas kernels: 48 us -> 43.9 us  [body(): pl.pallas_call(functools.partial(kernel, n_cell), out_shape=(jax.ShapeDty...]
where the time goes in v2:
time: 46.5 us; the launch traced here: 46.4 us
  Pallas kernels  45.7 us (98%)
  between operations  0.64 us (1%)
    pallas_call x1, Pallas kernels, body(): pl.pallas_call(functools.partial(kernel, n_cell), out_shape=(jax.ShapeDty...  43.9 us
    pallas_call x1, Pallas kernels, body(): pl.pallas_call(prolong, out_shape=(jax.ShapeDtypeStruct(fine_rows.shape,...  1.81 us

profile of v2, /device:TPU:1, one launch (start us, length us, event | category | flops | bytes accessed | tf_op | source)
XLA Modules:
  0.0 46.4 jit_solution(11723609649920599731)
XLA Ops:
  0.6 43.9 %multigrid.1 = (f32[3,4,1024]{2,1,0:T(4,128)}, f32[3,4,1024]{2,1,0:T(4,128)}) custom-call(f32[6,128,128]{2,1,0:T(8,128)} %bitcast.13, s32[64,128]{1,0:T(8,128)} %bitcast.14, s32[1,64]{1,0:T(1,128)} %rt.1, s32[1,192]{1,0:T(1,128)} %rl.1, s32[6,1024]{1,0:T(8,128)} %nb.1, f32[6,1024]{1,0:T(8,128)} %fw.1, f32[1,1024]{1,0:T(1,128)} %bitcast.16, f32[6,1024]{1,0:T(8,128)} %de.1), custom_call_target="tpu_custom_call" | custom-call | tf_op jit(solution)/shard_map/multigrid/pallas_call | solution.py:609
  44.6 1.8 %prolong.1 = (f32[6,128,128]{2,1,0:T(8,128)}, f32[6,2,1024]{2,1,0:T(2,128)}) custom-call(s32[64,128]{1,0:T(8,128)} %bitcast.15, f32[3,4,1024]{2,1,0:T(4,128)} %get-tuple-element.6.coarse, f32[3,4,1024]{2,1,0:T(4,128)} %get-tuple-element.7.blocks_x), custom_call_target="tpu_custom_call" | custom-call | tf_op jit(solution)/shard_map/prolong/pallas_call | solution.py:677

commit v3 on v2

--- a/solution.py
+++ b/solution.py
@@ -27,6 +27,7 @@
 BF16 = jnp.bfloat16
 T_Q, T_R, T_H, T_L, T_END = 0, 6, 12, 18, 24
 PLANE, CORES = 8, 2
+EARLY = 5
 
 
 def spectral_value(distance):
@@ -373,12 +374,16 @@
 
         lax.fori_loop(*(5 * tile for tile in lane_tiles), one, 0)
 
-    def local_part(x_all):
+    tiles = (SEND + cc) // 256
+
+    def keep(x_all):
         own_hi, own_lo = split2(x_all[:, SEND:])
         xh_v[0:16, :] = own_hi
         xh_v[16:32, :] = own_lo
         x_v[...] = x_all
-        for nt in range((SEND + cc) // 256):
+
+    def local_part(which):
+        for nt in which:
             lanes = pl.ds(256 * nt, 256)
             a = dot(xh_v[...], wh[0:cc, lanes])
             b = dot(xh_v[0:16, :], wl[0:cc, lanes])
@@ -414,7 +419,7 @@
 
     @pl.when(sweeping)
     def _():
-        def own_matrix():
+        def own_table():
             taken_all(nb_r, move_sem.at[1])
             taken_all(fw_r, move_sem.at[2])
             ids = [jnp.broadcast_to(nb_r[s : s + 1, :], (8, cc)) for s in range(NB)]
@@ -430,11 +435,11 @@
                 hi = face[s].astype(BF16).astype(F32)
                 table[T_H + s : T_H + s + 1, :] = hi[0:1]
                 table[T_L + s : T_L + s + 1, :] = (face[s] - hi).astype(BF16).astype(F32)[0:1]
-            build(table, (0, cc // BLK), SEND // BLK)
 
         @pl.when(jnp.logical_not(swapped))
         def _():
-            own_matrix()
+            own_table()
+            build(table, (0, EARLY), SEND // BLK)
 
         taken_all(lrx, list_sem.at[0])
         lane_slot = lax.broadcasted_iota(jnp.int32, (1, SEND), 1) // HS
@@ -476,28 +481,41 @@
         r_send = parts[0:16] + parts[16:32] + parts[32:48]
         x_send = r_send * di_v[:, 0:SEND]
         send_halo(0, x_send)
+        r_v[:, 0:SEND] = r_send
+        r_v[:, SEND:] = rest
+        keep(jnp.concatenate([x_send, rest * di_v[:, SEND:]], axis=1))
 
         @pl.when(swapped)
         def _():
-            own_matrix()
+            own_table()
 
         stable[...] = dot(table[...].astype(BF16), sel[...])
         build(stable, (0, SEND // BLK), 0)
-        r_v[:, 0:SEND] = r_send
-        r_v[:, SEND:] = rest
-        local_part(jnp.concatenate([x_send, rest * di_v[:, SEND:]], axis=1))
+        local_part((0,))
+
+        def own_sweep(rows, x_send):
+            local_part(range(1, tiles))
+            parts = [x_send]
+            for nt in range(cc // 256):
+                parts.append(with_halo(rows, pl.ds(SEND + 256 * nt, 256)))
+            keep(jnp.concatenate(parts, axis=1))
+            local_part((0,))
+
+        rows = halo_rows(0)
+        x_send = with_halo(rows, pl.ds(0, SEND))
+        send_halo(1, x_send)
+        build(table, (jnp.where(swapped, 0, EARLY), cc // BLK), SEND // BLK)
+        own_sweep(rows, x_send)
 
         def sweep(k, _):
             rows = halo_rows(k)
             x_send = with_halo(rows, pl.ds(0, SEND))
             send_halo(k + 1, x_send)
-            parts = [x_send]
-            for nt in range(cc // 256):
-                parts.append(with_halo(rows, pl.ds(SEND + 256 * nt, 256)))
-            local_part(jnp.concatenate(parts, axis=1))
+            own_sweep(rows, x_send)
             return 0
 
-        lax.fori_loop(0, ITERS - 1, sweep, 0)
+        lax.fori_loop(1, ITERS - 1, sweep, 0)
+        local_part(range(1, tiles))
         rows = halo_rows(ITERS - 1)
         for nt in (0, cc // 256 - 1, *range(1, cc // 256 - 1)):
             out = with_halo(rows, pl.ds(SEND + 256 * nt, 256))
@@ -609,8 +627,8 @@
     coarse, in_blocks = pl.pallas_call(
         functools.partial(kernel, n_cell),
         out_shape=(
-            jax.ShapeDtypeStruct((SWEEPERS, 4, cc), F32),
-            jax.ShapeDtypeStruct((SWEEPERS, 4, cc), F32),
+            pltpu.VMEM((SWEEPERS, 4, cc), F32),
+            pltpu.VMEM((SWEEPERS, 4, cc), F32),
         ),
         in_specs=[any_spec] * 8,
         out_specs=(out_spec, out_spec),
@@ -682,8 +700,13 @@
         ),
         in_specs=[out_spec] * 3,
         out_specs=(out_spec, out_spec),
+        compiler_params=pltpu.CompilerParams(vmem_limit_bytes=8 << 20),
         name="prolong",
-    )(cells_map, coarse, in_blocks)
+    )(
+        cells_map,
+        pltpu.with_memory_space_constraint(coarse, pltpu.VMEM),
+        pltpu.with_memory_space_constraint(in_blocks, pltpu.VMEM),
+    )
     fine = fine.reshape(var_count, blocks, inst_dev, BLK).transpose(2, 0, 1, 3).reshape(inst_dev, var_count, fine_dev)
     return fine, coarse.transpose(1, 0, 2)
 

time: 46.5 us -> 43.5 us (0.935)
  Pallas kernels: 45.7 us -> 42.7 us
    pallas_call x1, Pallas kernels: 43.9 us -> 41.7 us  [body(): pl.pallas_call(functools.partial(kernel, n_cell), out_shape=(pltpu.VMEM((...]
    pallas_call x1, Pallas kernels: 1.81 us -> 0.97 us  [body(): pl.pallas_call(prolong, out_shape=(jax.ShapeDtypeStruct(fine_rows.shape,...]
where the time goes in v3:
time: 43.5 us; the launch traced here: 43.4 us
  Pallas kernels  42.7 us (98%)
  between operations  0.66 us (2%)
    pallas_call x1, Pallas kernels, body(): pl.pallas_call(functools.partial(kernel, n_cell), out_shape=(pltpu.VMEM((...  41.7 us
    pallas_call x1, Pallas kernels, body(): pl.pallas_call(prolong, out_shape=(jax.ShapeDtypeStruct(fine_rows.shape,...  0.97 us

profile of v3, /device:TPU:1, one launch (start us, length us, event | category | flops | bytes accessed | tf_op | source)
XLA Modules:
  0.0 43.4 jit_solution(9328626876890349491)
XLA Ops:
  0.6 0.0 copy-start
  0.6 41.7 %multigrid.1 = (f32[3,4,1024]{2,1,0:T(4,128)S(1)}, f32[3,4,1024]{2,1,0:T(4,128)S(1)}) custom-call(f32[6,128,128]{2,1,0:T(8,128)} %bitcast.15, s32[64,128]{1,0:T(8,128)} %bitcast.13, s32[1,64]{1,0:T(1,128)} %rt.1, s32[1,192]{1,0:T(1,128)} %rl.1, s32[6,1024]{1,0:T(8,128)} %nb.1, f32[6,1024]{1,0:T(8,128)} %fw.1, f32[1,1024]{1,0:T(1,128)} %bitcast.16, f32[6,1024]{1,0:T(8,128)} %de.1), custom_call_target="tpu_custom_call" | custom-call | tf_op jit(solution)/shard_map/multigrid/pallas_call | solution.py:627
  42.4 0.0 copy-done
  42.4 1.0 %prolong.1 = (f32[6,128,128]{2,1,0:T(8,128)}, f32[6,2,1024]{2,1,0:T(2,128)}) custom-call(s32[64,128]{1,0:T(8,128)S(1)} %bitcast.14, f32[3,4,1024]{2,1,0:T(4,128)S(1)} %get-tuple-element.6.coarse, f32[3,4,1024]{2,1,0:T(4,128)S(1)} %get-tuple-element.7.blocks_x), custom_call_target="tpu_custom_call" | custom-call | tf_op jit(solution)/shard_map/prolong/pallas_call | solution.py:695
Async XLA Ops:
  0.6 41.8 %copy-start = (s32[8192]{0:T(1024)S(1)}, s32[8192]{0:T(1024)}, u32[]{:S(2)}) copy-start(s32[8192]{0:T(1024)} %param.9) | copy-start | bytes 98308

commit v4 on v3

--- a/solution.py
+++ b/solution.py
@@ -414,7 +414,7 @@
     def send_halo(k, x_send):
         xsend[k, 0] = x_send[:, 0:BLK]
         xsend[k, 1] = x_send[:, BLK:SEND]
-        for t in range(PEERS):
+        for t in (0, 5, 1, 4, 2, 3):
             halo_copy(k, t).start()
 
     @pl.when(sweeping)

time: 43.5 us -> 43.1 us (level)
  no operation moved by 1% of the time
where the time goes in v4:
time: 43.1 us; the launch traced here: 43 us
  Pallas kernels  42.4 us (98%)
  between operations  0.66 us (2%)
    pallas_call x1, Pallas kernels, body(): pl.pallas_call(functools.partial(kernel, n_cell), out_shape=(pltpu.VMEM((...  41.4 us
    pallas_call x1, Pallas kernels, body(): pl.pallas_call(prolong, out_shape=(jax.ShapeDtypeStruct(fine_rows.shape,...  0.97 us

profile of v4, /device:TPU:1, one launch (start us, length us, event | category | flops | bytes accessed | tf_op | source)
XLA Modules:
  0.0 43.0 jit_solution(8187530384073510020)
XLA Ops:
  0.6 0.0 copy-start
  0.6 41.4 %multigrid.1 = (f32[3,4,1024]{2,1,0:T(4,128)S(1)}, f32[3,4,1024]{2,1,0:T(4,128)S(1)}) custom-call(f32[6,128,128]{2,1,0:T(8,128)} %bitcast.15, s32[64,128]{1,0:T(8,128)} %bitcast.13, s32[1,64]{1,0:T(1,128)} %rt.1, s32[1,192]{1,0:T(1,128)} %rl.1, s32[6,1024]{1,0:T(8,128)} %nb.1, f32[6,1024]{1,0:T(8,128)} %fw.1, f32[1,1024]{1,0:T(1,128)} %bitcast.16, f32[6,1024]{1,0:T(8,128)} %de.1), custom_call_target="tpu_custom_call" | custom-call | tf_op jit(solution)/shard_map/multigrid/pallas_call | solution.py:627
  42.1 0.0 copy-done
  42.1 1.0 %prolong.1 = (f32[6,128,128]{2,1,0:T(8,128)}, f32[6,2,1024]{2,1,0:T(2,128)}) custom-call(s32[64,128]{1,0:T(8,128)S(1)} %bitcast.14, f32[3,4,1024]{2,1,0:T(4,128)S(1)} %get-tuple-element.6.coarse, f32[3,4,1024]{2,1,0:T(4,128)S(1)} %get-tuple-element.7.blocks_x), custom_call_target="tpu_custom_call" | custom-call | tf_op jit(solution)/shard_map/prolong/pallas_call | solution.py:695
Async XLA Ops:
  0.6 41.4 %copy-start = (s32[8192]{0:T(1024)S(1)}, s32[8192]{0:T(1024)}, u32[]{:S(2)}) copy-start(s32[8192]{0:T(1024)} %param.9) | copy-start | bytes 98308

commit v5 on v4

--- a/solution.py
+++ b/solution.py
@@ -293,7 +293,7 @@
 
     @pl.when(sweeping)
     def _():
-        for t in range(PEERS):
+        for t in (0, 5, 1, 4, 2, 3):
             if abs(OFFSETS[t]) == 2:
                 here = mirror(wrap(cell + OFFSETS[t])) == cell
 

time: 43.1 us -> 43.1 us (level)
  no operation moved by 1% of the time
where the time goes in v5:
time: 43.1 us; the launch traced here: 43 us
  Pallas kernels  42.4 us (98%)
  between operations  0.66 us (2%)
    pallas_call x1, Pallas kernels, body(): pl.pallas_call(functools.partial(kernel, n_cell), out_shape=(pltpu.VMEM((...  41.4 us
    pallas_call x1, Pallas kernels, body(): pl.pallas_call(prolong, out_shape=(jax.ShapeDtypeStruct(fine_rows.shape,...  0.97 us

profile of v5, /device:TPU:1, one launch (start us, length us, event | category | flops | bytes accessed | tf_op | source)
XLA Modules:
  0.0 43.0 jit_solution(240129473541972446)
XLA Ops:
  0.6 0.0 copy-start
  0.6 41.4 %multigrid.1 = (f32[3,4,1024]{2,1,0:T(4,128)S(1)}, f32[3,4,1024]{2,1,0:T(4,128)S(1)}) custom-call(f32[6,128,128]{2,1,0:T(8,128)} %bitcast.15, s32[64,128]{1,0:T(8,128)} %bitcast.13, s32[1,64]{1,0:T(1,128)} %rt.1, s32[1,192]{1,0:T(1,128)} %rl.1, s32[6,1024]{1,0:T(8,128)} %nb.1, f32[6,1024]{1,0:T(8,128)} %fw.1, f32[1,1024]{1,0:T(1,128)} %bitcast.16, f32[6,1024]{1,0:T(8,128)} %de.1), custom_call_target="tpu_custom_call" | custom-call | tf_op jit(solution)/shard_map/multigrid/pallas_call | solution.py:627
  42.1 0.0 copy-done
  42.1 1.0 %prolong.1 = (f32[6,128,128]{2,1,0:T(8,128)}, f32[6,2,1024]{2,1,0:T(2,128)}) custom-call(s32[64,128]{1,0:T(8,128)S(1)} %bitcast.14, f32[3,4,1024]{2,1,0:T(4,128)S(1)} %get-tuple-element.6.coarse, f32[3,4,1024]{2,1,0:T(4,128)S(1)} %get-tuple-element.7.blocks_x), custom_call_target="tpu_custom_call" | custom-call | tf_op jit(solution)/shard_map/prolong/pallas_call | solution.py:695
Async XLA Ops:
  0.6 41.4 %copy-start = (s32[8192]{0:T(1024)S(1)}, s32[8192]{0:T(1024)}, u32[]{:S(2)}) copy-start(s32[8192]{0:T(1024)} %param.9) | copy-start | bytes 98308
